TPU v7x, 32 devices: a whole 2x2x4 slice. The times are simulated.
32 devices in a mesh: dp: 8 (over z, y), tensor: 4 (over x, core).
Axes of the slice: x: 2, y: 2, z: 4, core: 2. Of those that a mesh axis runs over, the one named last changes fastest.
Arguments:
- hidden: bfloat16 [2048, 18432], P('dp', 'tensor'), may hold values from -6 to 6
- down_weight: bfloat16 [18432, 4608], P('tensor', 'dp'), may hold values from -0.046875 to 0.046875
- residual: bfloat16 [2048, 4608], P('dp'), may hold values from -6 to 6
- post_gain: float32 [4608], replicated, may hold values from 0.5 to 1.5
- pre_gain: float32 [4608], replicated, may hold values from 0.5 to 1.5
- cast_scale: float32 [1], replicated, may hold values from 100 to 400
- amax_history: float32 [3, 1024], replicated, may hold values from 0.25 to 4
Outputs:
- cast_out: bfloat16 [2048, 4608], P('dp')
- residual_out: bfloat16 [2048, 4608], P('dp')
- peaks: float32 [3], replicated
- new_history: float32 [3, 1024], replicated
- new_scales: float32 [3], replicated
All inputs are finite; a program needn't handle non-finite values.
Results may differ from a plain program's by a relative error of at most 0.012.
Values may be sent and summed in bfloat16 or wider, within the bound.
A program may use at most 128 MiB of HBM per device.

v0:
```python
import jax
import jax.numpy as jnp
from jax import lax
from jax.sharding import PartitionSpec as P

norm_epsilon = 1e-06
float_limit = 448.0


def rms_norm(values, gain_vector):
    return (
        values
        * lax.rsqrt(jnp.mean(values * values, axis=-1, keepdims=True) + norm_epsilon)
        * gain_vector
    )


def finish(summed, stream_in, post_gain, pre_gain, stale_scale):
    stream = stream_in.astype(jnp.float32) + rms_norm(summed, post_gain)
    normed = rms_norm(stream, pre_gain)
    cast_rows = (jnp.clip(normed * stale_scale, -float_limit, float_limit) / stale_scale).astype(
        jnp.bfloat16
    )
    peak_values = jnp.stack(
        [jnp.max(jnp.abs(summed)), jnp.max(jnp.abs(stream)), jnp.max(jnp.abs(normed))]
    )
    return (cast_rows, stream.astype(jnp.bfloat16), peak_values)


def on_device(hidden, down_weight, residual, post_gain, pre_gain, cast_scale, amax_history):
    stale_scale = cast_scale[0]
    partial_value = jnp.dot(
        lax.all_gather(hidden, "dp", axis=0, tiled=True),
        down_weight,
        preferred_element_type=jnp.float32,
    )
    column_total = lax.psum(partial_value.astype(jnp.bfloat16), "tensor").astype(jnp.float32)
    summed = lax.all_to_all(
        column_total.astype(jnp.bfloat16), "dp", split_axis=0, concat_axis=1, tiled=True
    ).astype(column_total.dtype)
    cast_out, residual_out, peak_values = finish(summed, residual, post_gain, pre_gain, stale_scale)
    peak_values = lax.pmax(peak_values, ("dp", "tensor"))
    new_history = jnp.concatenate([peak_values[:, None], amax_history[:, :-1]], axis=1)
    new_scales = float_limit / jnp.maximum(jnp.max(new_history, axis=1), 1.0)
    return (cast_out, residual_out, peak_values, new_history, new_scales)


def solution(mesh):
    in_specs = (P("dp", "tensor"), P("tensor", "dp"), P("dp", None), P(), P(), P(), P())
    out_specs = (P("dp", None), P("dp", None), P(), P(), P())
    return jax.shard_map(
        on_device, mesh=mesh, in_specs=in_specs, out_specs=out_specs, check_vma=False
    )
```

profile of v0, /device:TPU:10, one launch (start us, length us, event | category | flops | bytes accessed | tf_op | source)
XLA Modules:
  0.0 571.8 jit_solution(3271551437250830169)
XLA Ops:
  7.2 0.0 all-gather.2.cloned.1.call-start
  7.2 0.7 all-gather.2.cloned.1.call-update
  7.9 0.0 all-reduce.2.cloned.1.call-start
  7.9 365.1 %all-gather.2.cloned.1.call-done = bf16[2048,4608]{1,0:T(8,128)(2,1)} async-done(((bf16[256,4608]{1,0:T(8,128)(2,1)}), bf16[2048,4608]{1,0:T(8,128)(2,1)}) %all-gather.2.cloned.1.call-update) | async-done | bytes 18874384 | tf_op jit(solution)/shard_map/all_gather | solution.py:33
  373.0 16.5 %convolution_convert_fusion = bf16[2048,576]{0,1:T(8,128)(2,1)S(1)} fusion(bf16[2048,4608]{1,0:T(8,128)(2,1)} %all-gather.2.cloned.1.call-done, bf16[4608,576]{0,1:T(8,128)(2,1)} %param.8), kind=kOutput, calls=%fused_computation.10 | convolution fusion | flops 10872815616 | bytes 26542080 | tf_op jit(solution)/shard_map/dot_general | solution.py:32
  389.6 1.6 copy.21
  391.2 0.0 all-reduce.2.cloned.1.call-update
  391.2 55.0 %all-reduce.2.cloned.1.call-done = bf16[8,256,576]{1,2,0:T(8,128)(2,1)} async-done(((bf16[8,256,576]{1,2,0:T(8,128)(2,1)}), bf16[8,256,576]{1,2,0:T(8,128)(2,1)}) %all-reduce.2.cloned.1.call-update) | async-done | bytes 2359312 | tf_op jit(solution)/shard_map/psum | solution.py:37
  446.1 6.1 %all-to-all-start = ((bf16[8,256,576]{1,2,0:T(8,128)(2,1)}), bf16[8,256,576]{1,2,0:T(8,128)(2,1)S(1)}, u32[]{:S(2)}, u32[]{:S(2)}) async-start(bf16[8,256,576]{1,2,0:T(8,128)(2,1)} %all-reduce.2.cloned.1.call-done), calls=%async_computation | async-start | bytes 4718592 | tf_op jit(solution)/shard_map/all_to_all | solution.py:38
  452.2 0.0 copy-start.2
  452.2 4.3 copy.14
  456.5 0.0 copy-start.3
  457.1 46.4 %all-to-all-done = bf16[8,256,576]{1,2,0:T(8,128)(2,1)S(1)} async-done(((bf16[8,256,576]{1,2,0:T(8,128)(2,1)}), bf16[8,256,576]{1,2,0:T(8,128)(2,1)S(1)}, u32[]{:S(2)}, u32[]{:S(2)}) %all-to-all-start) | async-done | bytes 2359328 | tf_op jit(solution)/shard_map/all_to_all | solution.py:38
  503.5 0.0 copy-start
  503.5 1.2 abs_reduce_fusion.2
  504.7 0.0 copy-done.2
  504.7 3.3 multiply_reduce_fusion
  508.0 0.0 copy-done.3
  508.0 0.0 copy-done
  508.0 0.0 copy-start.4
  508.1 4.8 abs_reduce_fusion.1
  512.8 0.0 copy-start.1
  512.8 2.2 pad_maximum_fusion.1
  515.0 0.0 copy-done.4
  515.0 0.1 slice_reduce_fusion
  515.1 41.9 %pmax.7 = f32[3]{0:T(128)S(1)} all-reduce(f32[3]{0:T(128)S(1)} %pad_maximum_fusion.1), channel_id=1, replica_groups=mesh['dp'=8,'tensor'=4] {'dp','tensor'}, use_global_device_ids=true, to_apply=%region_6.7 | all-reduce | flops 3 | bytes 24 | tf_op jit(solution)/shard_map/pmax | solution.py:42
  557.0 0.0 copy-start.5
  557.0 0.1 copy.16
  557.1 0.5 maximum_divide_fusion
  557.6 4.3 copy.17
  561.9 0.0 copy-done.1
  561.9 2.4 copy.18
  564.3 0.0 copy-done.5
  564.3 0.7 pad_maximum_fusion
  (2 shorter events, 0.0 us)
Async XLA Ops:
  7.2 365.9 %all-gather.2.cloned.1.call-start = ((), (), s32[]{:S(2)}) async-start(), calls=%async_computation.1 | async-start | bytes 21233664 | tf_op jit(solution)/shard_map/all_gather | solution.py:33
  7.9 438.2 %all-reduce.2.cloned.1.call-start = ((), (), s32[]{:S(2)}) async-start(), calls=%async_computation.2 | async-start | bytes 4718592 | tf_op jit(solution)/shard_map/psum | solution.py:37
  446.1 57.4 %all-to-all-start = ((bf16[8,256,576]{1,2,0:T(8,128)(2,1)}), bf16[8,256,576]{1,2,0:T(8,128)(2,1)S(1)}, u32[]{:S(2)}, u32[]{:S(2)}) async-start(bf16[8,256,576]{1,2,0:T(8,128)(2,1)} %all-reduce.2.cloned.1.call-done), calls=%async_computation | async-start | bytes 4718592 | tf_op jit(solution)/shard_map/all_to_all | solution.py:38
  452.2 52.5 %copy-start.2 = (f32[4608]{0:T(1024)S(1)}, f32[4608]{0:T(1024)}, u32[]{:S(2)}) copy-start(f32[4608]{0:T(1024)} %param.10) | copy-start | bytes 55300
  456.5 51.5 %copy-start.3 = (f32[4608]{0:T(1024)S(1)}, f32[4608]{0:T(1024)}, u32[]{:S(2)}) copy-start(f32[4608]{0:T(1024)} %param.11) | copy-start | bytes 55300
  503.5 4.5 copy-start
  508.0 7.0 %copy-start.4 = (f32[3,1024]{1,0:T(4,128)S(1)}, f32[3,1024]{1,0:T(4,128)}, u32[]{:S(2)}) copy-start(f32[3,1024]{1,0:T(4,128)} %param.13) | copy-start | bytes 36868
  512.8 49.0 %copy-start.1 = (bf16[256,4608]{0,1:T(8,128)(2,1)S(1)}, bf16[256,4608]{0,1:T(8,128)(2,1)}, u32[]{:S(2)}) copy-start(bf16[256,4608]{0,1:T(8,128)(2,1)} %get-tuple-element.15) | copy-start | bytes 7077892
  557.0 7.3 %copy-start.5 = (f32[3]{0:T(128)}, f32[3]{0:T(128)S(1)}, u32[]{:S(2)}) copy-start(f32[3]{0:T(128)S(1)} %pmax.7) | copy-start | bytes 40
Sparse Core Ops, SparseCore 0:
  9.5 363.4 all-gather.1
  391.3 54.8 all-reduce.1
where the time goes:
time: 572 us
  waiting for transfers between devices  467 us (82%)
  blocking collectives  41.9 us (7%)
  matrix products  16.5 us (3%)
  between operations  14.7 us (3%)
  other arithmetic  12.8 us (2%)
  local copies, waits for them, and re-layouts  12.6 us (2%)
  starting transfers between devices  6.13 us (1%)
    all_gather x1, waiting for transfers between devices, on_device(): lax.all_gather(hidden, 'dp', axis=0, tiled=True)  365 us
    psum x1, waiting for transfers between devices, on_device(): lax.psum(partial_value.astype(jnp.bfloat16), 'tensor').astype(jnp.float32)  55 us
    all_to_all x1, waiting for transfers between devices, on_device(): lax.all_to_all(column_total.astype(jnp.bfloat16), 'dp', split_axis=0, con...  46.4 us
    pmax x1, blocking collectives, on_device(): peak_values = lax.pmax(peak_values, ('dp', 'tensor'))  41.9 us
    dot_general x1, matrix products, on_device(): jnp.dot(lax.all_gather(hidden, 'dp', axis=0, tiled=True), down_weight, pr...  16.5 us
  transfers between devices with their start and end apart: 3, of which 3 were waited for; matrix products, arithmetic and copies ran while one was open for 1% of the time, Pallas kernels for 0%

commit v1 on v0

--- a/solution.py
+++ b/solution.py
@@ -34,7 +34,9 @@
         down_weight,
         preferred_element_type=jnp.float32,
     )
-    column_total = lax.psum(partial_value.astype(jnp.bfloat16), "tensor").astype(jnp.float32)
+    column_total = jnp.sum(
+        lax.all_gather(partial_value.astype(jnp.bfloat16), "tensor"), axis=0
+    ).astype(jnp.float32)
     summed = lax.all_to_all(
         column_total.astype(jnp.bfloat16), "dp", split_axis=0, concat_axis=1, tiled=True
     ).astype(column_total.dtype)

time: 572 us -> 612 us (1.070)
  local copies, waits for them, and re-layouts: 12.6 us -> 28.8 us
  other arithmetic: 12.8 us -> 26.1 us
  waiting for transfers between devices: 467 us -> 476 us
    all_gather x0 -> x1, waiting for transfers between devices: none -> 63.5 us  [on_device(): lax.all_gather(partial_value.astype(jnp.bfloat16), 'tensor')]
    psum x1 -> x0, waiting for transfers between devices: 55 us -> none  [on_device(): lax.psum(partial_value.astype(jnp.bfloat16), 'tensor').astype(jnp.float32)]
    all_gather x0 -> x1, local copies, waits for them, and re-layouts: none -> 16.2 us  [on_device(): lax.all_gather(partial_value.astype(jnp.bfloat16), 'tensor')]
    reduce_sum x0 -> x1, other arithmetic: none -> 13.2 us  [on_device(): jnp.sum(lax.all_gather(partial_value.astype(jnp.bfloat16), 'tensor'), axi...]
where the time goes in v1:
time: 612 us; the launch traced here: 611 us
  waiting for transfers between devices  476 us (78%)
  blocking collectives  41.9 us (7%)
  local copies, waits for them, and re-layouts  28.8 us (5%)
  other arithmetic  26.1 us (4%)
  matrix products  17.5 us (3%)
  between operations  14.7 us (2%)
  starting transfers between devices  6.13 us (1%)
    all_gather x1, waiting for transfers between devices, on_device(): lax.all_gather(hidden, 'dp', axis=0, tiled=True)  365 us
    all_gather x1, waiting for transfers between devices, on_device(): lax.all_gather(partial_value.astype(jnp.bfloat16), 'tensor')  63.5 us
    all_to_all x1, waiting for transfers between devices, on_device(): lax.all_to_all(column_total.astype(jnp.bfloat16), 'dp', split_axis=0, con...  46.9 us
    pmax x1, blocking collectives, on_device(): peak_values = lax.pmax(peak_values, ('dp', 'tensor'))  41.9 us
    dot_general x1, matrix products, on_device(): jnp.dot(lax.all_gather(hidden, 'dp', axis=0, tiled=True), down_weight, pr...  17.5 us
    all_gather x1, local copies, waits for them, and re-layouts, on_device(): lax.all_gather(partial_value.astype(jnp.bfloat16), 'tensor')  16.2 us
    reduce_sum x1, other arithmetic, on_device(): jnp.sum(lax.all_gather(partial_value.astype(jnp.bfloat16), 'tensor'), axi...  13.2 us
  transfers between devices with their start and end apart: 3, of which 3 were waited for; matrix products, arithmetic and copies ran while one was open for 1% of the time, Pallas kernels for 0%

profile of v1, /device:TPU:10, one launch (start us, length us, event | category | flops | bytes accessed | tf_op | source)
XLA Modules:
  0.0 611.4 jit_solution(7275621182953503239)
XLA Ops:
  7.2 0.0 all-gather.4.cloned.1.call-start
  7.2 0.7 all-gather.4.cloned.1.call-update
  7.9 0.0 all-gather.6.cloned.1.call-start
  7.9 365.1 %all-gather.4.cloned.1.call-done = bf16[2048,4608]{1,0:T(8,128)(2,1)} async-done(((bf16[256,4608]{1,0:T(8,128)(2,1)}), bf16[2048,4608]{1,0:T(8,128)(2,1)}) %all-gather.4.cloned.1.call-update) | async-done | bytes 18874384 | tf_op jit(solution)/shard_map/all_gather | solution.py:33
  373.0 17.5 %convolution_convert_fusion = bf16[2048,576]{0,1:T(8,128)(2,1)} fusion(bf16[2048,4608]{1,0:T(8,128)(2,1)} %all-gather.4.cloned.1.call-done, bf16[4608,576]{0,1:T(8,128)(2,1)} %param.8), kind=kOutput, calls=%fused_computation.10 | convolution fusion | flops 10872815616 | bytes 26542080 | tf_op jit(solution)/shard_map/dot_general | solution.py:32
  390.6 0.0 all-gather.6.cloned.1.call-update
  390.6 63.5 %all-gather.6.cloned.1.call-done = bf16[8192,576]{0,1:T(8,128)(2,1)} async-done(((bf16[2048,576]{0,1:T(8,128)(2,1)}), bf16[8192,576]{0,1:T(8,128)(2,1)}) %all-gather.6.cloned.1.call-update) | async-done | bytes 9437200 | tf_op jit(solution)/shard_map/all_gather | solution.py:38
  454.1 16.2 %reshape.36 = bf16[4,2048,576]{1,0,2:T(4,128)(2,1)} reshape(bf16[8192,576]{0,1:T(8,128)(2,1)} %all-gather.6.cloned.1.call-done) | data formatting | bytes 18874368 | tf_op jit(solution)/shard_map/all_gather | solution.py:38
  470.2 13.2 %reduce_sum.30 = bf16[2048,576]{0,1:T(8,128)(2,1)S(1)} reduce(bf16[4,2048,576]{1,0,2:T(4,128)(2,1)} %reshape.36, bf16[]{:T(256)} %constant.4.clone.1), dimensions={0}, to_apply=%region_0.0 | reduce | flops 3538944 | bytes 11796482 | tf_op jit(solution)/shard_map/reduce_sum | solution.py:37
  483.5 1.6 copy.25
  485.0 6.1 all-to-all-start
  491.1 0.0 copy-start.2
  491.1 4.3 copy.18
  495.4 0.0 copy-start.3
  496.0 46.9 %all-to-all-done = bf16[8,256,576]{1,2,0:T(8,128)(2,1)S(1)} async-done(((bf16[8,256,576]{1,2,0:T(8,128)(2,1)}), bf16[8,256,576]{1,2,0:T(8,128)(2,1)S(1)}, u32[]{:S(2)}, u32[]{:S(2)}) %all-to-all-start) | async-done | bytes 2359328 | tf_op jit(solution)/shard_map/all_to_all | solution.py:40
  542.9 0.0 copy-start
  542.9 1.2 abs_reduce_fusion.2
  544.1 0.0 copy-done.2
  544.1 3.3 multiply_reduce_fusion
  547.5 0.0 copy-done.3
  547.5 0.0 copy-done
  547.5 0.0 copy-start.4
  547.5 4.8 abs_reduce_fusion.1
  552.3 0.0 copy-start.1
  552.3 2.2 pad_maximum_fusion.1
  554.5 0.0 copy-done.4
  554.5 0.1 slice_reduce_fusion
  554.6 41.9 %pmax.7 = f32[3]{0:T(128)S(1)} all-reduce(f32[3]{0:T(128)S(1)} %pad_maximum_fusion.1), channel_id=1, replica_groups=mesh['dp'=8,'tensor'=4] {'dp','tensor'}, use_global_device_ids=true, to_apply=%region_6.7 | all-reduce | flops 3 | bytes 24 | tf_op jit(solution)/shard_map/pmax | solution.py:44
  596.5 0.0 copy-start.5
  596.5 0.1 copy.20
  596.6 0.5 maximum_divide_fusion
  597.1 4.3 copy.21
  601.4 0.0 copy-done.1
  601.4 2.4 copy.22
  603.8 0.0 copy-done.5
  603.8 0.7 pad_maximum_fusion
  (2 shorter events, 0.0 us)
Async XLA Ops:
  7.2 365.9 %all-gather.4.cloned.1.call-start = ((), (), s32[]{:S(2)}) async-start(), calls=%async_computation.1 | async-start | bytes 21233664 | tf_op jit(solution)/shard_map/all_gather | solution.py:33
  7.9 446.2 %all-gather.6.cloned.1.call-start = ((), (), s32[]{:S(2)}) async-start(), calls=%async_computation.2 | async-start | bytes 11796480 | tf_op jit(solution)/shard_map/all_gather | solution.py:38
  485.0 57.9 %all-to-all-start = ((bf16[8,256,576]{1,2,0:T(8,128)(2,1)}), bf16[8,256,576]{1,2,0:T(8,128)(2,1)S(1)}, u32[]{:S(2)}, u32[]{:S(2)}) async-start(bf16[8,256,576]{1,2,0:T(8,128)(2,1)} %bitcast.32), calls=%async_computation | async-start | bytes 4718592 | tf_op jit(solution)/shard_map/all_to_all | solution.py:40
  491.1 53.0 %copy-start.2 = (f32[4608]{0:T(1024)S(1)}, f32[4608]{0:T(1024)}, u32[]{:S(2)}) copy-start(f32[4608]{0:T(1024)} %param.10) | copy-start | bytes 55300
  495.4 52.1 %copy-start.3 = (f32[4608]{0:T(1024)S(1)}, f32[4608]{0:T(1024)}, u32[]{:S(2)}) copy-start(f32[4608]{0:T(1024)} %param.11) | copy-start | bytes 55300
  542.9 4.6 copy-start
  547.5 7.0 %copy-start.4 = (f32[3,1024]{1,0:T(4,128)S(1)}, f32[3,1024]{1,0:T(4,128)}, u32[]{:S(2)}) copy-start(f32[3,1024]{1,0:T(4,128)} %param.13) | copy-start | bytes 36868
  552.3 49.1 %copy-start.1 = (bf16[256,4608]{0,1:T(8,128)(2,1)S(1)}, bf16[256,4608]{0,1:T(8,128)(2,1)}, u32[]{:S(2)}) copy-start(bf16[256,4608]{0,1:T(8,128)(2,1)} %get-tuple-element.20) | copy-start | bytes 7077892
  596.5 7.3 %copy-start.5 = (f32[3]{0:T(128)}, f32[3]{0:T(128)S(1)}, u32[]{:S(2)}) copy-start(f32[3]{0:T(128)S(1)} %pmax.7) | copy-start | bytes 40
Sparse Core Ops, SparseCore 0:
  9.5 363.4 all-gather.3
  390.7 63.2 all-gather.5
